TPU v7x, 32 devices: a whole 2x2x4 slice. The times are simulated.
32 devices in a mesh: wide: 16 (over z, y, x), narrow: 2 (over core).
Axes of the slice: x: 2, y: 2, z: 4, core: 2. Of those that a mesh axis runs over, the one named last changes fastest.
Arguments:
- contributions: float32 [2, 3, 8192, 128], P('narrow', None, 'wide'), may hold values from -6 to 6
- send_map: int32 [16, 800], P('wide'), may hold values from -1 to 511, as said below
- arrival_map: int32 [16, 800], P('wide'), may hold values from -1 to 255, as said below
- dual_diagonal: float32 [4096, 128], P('wide'), may hold values from 0.5 to 2
- mortar: bfloat16 [4096, 128, 128], P('wide'), may hold values from -0.5 to 0.5
- master_inverse: bfloat16 [4096, 128, 128], P('wide'), may hold values from -0.5 to 0.5
Outputs:
- corrections: float32 [2, 3, 8192, 128], P('narrow', None, 'wide')
Inputs may be any that keep to these rules, and one draw needn't show every extreme that they name: `send_map`: each row 0 to 511 of a partition stands in exactly one of its slots. Some stripe has all 50 of its slots used by every partition. arrival_map[d, o * 50 + c] is -1 exactly where send_map[o, d * 50 + c] is -1.
All inputs are finite; a program needn't handle non-finite values.
Results may differ from a plain program's by a relative error of at most 0.0041.
Values sent between devices are 32-bit elements; how exact they have to be, the bound alone decides.
A program may use at most 64 MiB of HBM per device.

v0:
```python
import functools

import jax
import jax.numpy as jnp
from jax import lax
from jax.experimental import pallas as pl
from jax.experimental.pallas import tpu as pltpu
from jax.sharding import PartitionSpec as P

GROUP = 16
SUBLANES = 8


def one_hot_dot(mask, values):
    high = values.astype(jnp.bfloat16)
    low = (values - high.astype(jnp.float32)).astype(jnp.bfloat16)
    return jnp.dot(mask, high, preferred_element_type=jnp.float32) + jnp.dot(
        mask, low, preferred_element_type=jnp.float32
    )


def block_products(vectors, matrices, transposed):
    rows = lax.broadcasted_iota(jnp.int32, vectors.shape, 0)
    total = jnp.zeros(vectors.shape, jnp.float32)
    for b in range(vectors.shape[0]):
        product = lax.dot_general(
            vectors,
            matrices(b),
            (((1,), (1 if transposed else 0,)), ((), ())),
            preferred_element_type=jnp.float32,
        )
        total = jnp.where(rows == b, product, total)
    return total


def kernel(
    n,
    cap,
    contributions,
    send_col,
    send_row,
    arrival_col,
    arrival_row,
    diagonal,
    mortar_hbm,
    inverse_hbm,
    out,
    pick_mask,
    sum_mask,
    spread_mask,
    place_mask,
    going,
    coming,
    returning,
    returned,
    sums,
    other_sums,
    other_fix,
    fixes,
    mortar,
    inverse,
    fetch_sem,
    wide_send,
    wide_recv,
    pair_send,
    pair_recv,
):
    me = lax.axis_index("wide")
    side = lax.axis_index("narrow")
    comps, row_count, nodes = out.shape[1:]
    capp = coming.shape[2]
    slots = n * capp
    half = mortar.shape[0]

    fetches = [
        pltpu.make_async_copy(mortar_hbm.at[pl.ds(side * half, half)], mortar, fetch_sem.at[0]),
        pltpu.make_async_copy(inverse_hbm.at[pl.ds(side * half, half)], inverse, fetch_sem.at[1]),
    ]

    if capp > cap:
        last = pl.ds(capp - SUBLANES, SUBLANES)
        empty = jnp.zeros((comps, n, SUBLANES, nodes), jnp.float32)
        coming[:, :, last, :] = empty
        returned[:, :, last, :] = empty

    barrier = pltpu.get_barrier_semaphore()

    def greet(k, carry):
        pl.semaphore_signal(barrier, inc=1, device_id={"wide": lax.rem(me + k, n)}, device_id_type=pl.DeviceIdType.MESH)
        return carry

    lax.fori_loop(1, n, greet, 0)
    pl.semaphore_signal(barrier, inc=1, device_id={"narrow": 1 - side}, device_id_type=pl.DeviceIdType.MESH)
    for fetch in fetches:
        fetch.start()


    def mask_of(ids, shape, axis):
        return jnp.where(ids == lax.broadcasted_iota(jnp.int32, shape, axis), 1.0, 0.0).astype(jnp.bfloat16)

    def row_mask_of(ids, shape):
        tiles = (shape[0] // SUBLANES, SUBLANES, shape[1])
        rows = lax.broadcasted_iota(jnp.int32, tiles, 0) * SUBLANES + lax.broadcasted_iota(
            jnp.int32, tiles, 1
        )
        return jnp.where(ids[None] == rows, 1.0, 0.0).reshape(shape).astype(jnp.bfloat16)

    pick_mask[...] = mask_of(send_col[...], pick_mask.shape, 1)

    def exchange(source, target, c, phase):
        def one_copy(peer):
            pltpu.make_async_remote_copy(
                src_ref=source.at[c, peer, pl.ds(0, cap)],
                dst_ref=target.at[c, me, pl.ds(0, cap)],
                send_sem=wide_send.at[phase, c],
                recv_sem=wide_recv.at[phase, c],
                device_id={"wide": peer},
                device_id_type=pl.DeviceIdType.MESH,
            ).start()

        middle = n // 2
        one_copy(lax.rem(me + middle, n))

        def pair(k, carry):
            one_copy(lax.rem(me + middle + k, n))
            one_copy(lax.rem(me + middle - k, n))
            return carry

        lax.fori_loop(1, middle, pair, 0)

    def whole(ref, c, sem):
        view = ref.at[c, pl.ds(0, n - 1), pl.ds(0, cap)]
        return pltpu.make_async_copy(view, view, sem)

    for c in range(comps):
        going[c] = one_hot_dot(pick_mask[...], contributions[0, c]).reshape(n, capp, nodes)
        if c == 0:
            pl.semaphore_wait(barrier, n)
        exchange(going, coming, c, 0)
        coming[c, me] = going[c, me]

    sum_mask[...] = row_mask_of(arrival_row[...], sum_mask.shape)
    spread_mask[...] = mask_of(arrival_col[...], spread_mask.shape, 1)
    place_mask[...] = row_mask_of(send_row[...], place_mask.shape)

    mine = pl.multiple_of(side * half, half)
    theirs = pl.multiple_of((1 - side) * half, half)
    is_slave = side == 0

    for c in range(comps):
        whole(coming, c, wide_recv.at[0, c]).wait()
        sums[c] = one_hot_dot(sum_mask[...], coming[c].reshape(slots, nodes))
        swap = pltpu.make_async_remote_copy(
            src_ref=sums.at[c, pl.ds(theirs, half)],
            dst_ref=other_sums.at[c],
            send_sem=pair_send.at[0, c],
            recv_sem=pair_recv.at[0, c],
            device_id={"narrow": 1 - side},
            device_id_type=pl.DeviceIdType.MESH,
        )
        swap.start()
        if c == 0:
            for fetch in fetches:
                fetch.wait()
        swap.wait()

        def condense(g, carry):
            first = pl.multiple_of(g * GROUP, GROUP)
            rows = pl.ds(first, GROUP)
            own = sums[c, pl.ds(pl.multiple_of(mine + first, GROUP), GROUP), :]
            other = other_sums[c, rows, :]
            slave = jnp.where(is_slave, own, other)
            master = jnp.where(is_slave, other, own)
            scale = diagonal[pl.ds(pl.multiple_of(mine + first, GROUP), GROUP), :]
            low = (slave / scale).astype(jnp.bfloat16)
            condensed = master + block_products(low, lambda b: mortar[first + b], False)
            master_fix = block_products(
                condensed.astype(jnp.bfloat16), lambda b: inverse[first + b], True
            )
            slave_fix = (
                block_products(master_fix.astype(jnp.bfloat16), lambda b: mortar[first + b], True)
                / scale
            )
            fixes[c, pl.ds(pl.multiple_of(mine + first, GROUP), GROUP), :] = jnp.where(
                is_slave, slave_fix, master_fix
            )
            other_fix[c, rows, :] = jnp.where(is_slave, master_fix, slave_fix)
            return carry

        lax.fori_loop(0, half // GROUP, condense, 0, unroll=2)
        back = pltpu.make_async_remote_copy(
            src_ref=other_fix.at[c],
            dst_ref=fixes.at[c, pl.ds(mine, half)],
            send_sem=pair_send.at[1, c],
            recv_sem=pair_recv.at[1, c],
            device_id={"narrow": 1 - side},
            device_id_type=pl.DeviceIdType.MESH,
        )
        back.start()
        back.wait()
        returning[c] = one_hot_dot(spread_mask[...], fixes[c]).reshape(n, capp, nodes)
        exchange(returning, returned, c, 1)
        returned[c, me] = returning[c, me]

    for c in range(comps):
        whole(returned, c, wide_recv.at[1, c]).wait()
        out[0, c] = one_hot_dot(place_mask[...], returned[c].reshape(slots, nodes))
    for c in range(comps):
        whole(going, c, wide_send.at[0, c]).wait()
        whole(returning, c, wide_send.at[1, c]).wait()


def shards(contributions, send_map, arrival_map, dual_diagonal, mortar, master_inverse):
    n = lax.axis_size("wide")
    _, comps, row_count, nodes = contributions.shape
    blocks = dual_diagonal.shape[0]
    half = blocks // lax.axis_size("narrow")
    cap = send_map.shape[1] // n
    capp = -(-cap // SUBLANES) * SUBLANES
    slots = n * capp

    def padded(ids):
        return jnp.pad(
            ids.reshape(n, cap), ((0, 0), (0, capp - cap)), constant_values=-1
        )

    send = padded(send_map)
    arrival = padded(arrival_map)
    f32, bf16 = jnp.float32, jnp.bfloat16
    vmem = pl.BlockSpec(memory_space=pltpu.VMEM)
    hbm = pl.BlockSpec(memory_space=pl.ANY)
    travel = pltpu.VMEM((comps, n, capp, nodes), f32)
    return pl.pallas_call(
        functools.partial(kernel, n, cap),
        out_shape=jax.ShapeDtypeStruct((1, comps, row_count, nodes), f32),
        in_specs=[vmem] * 6 + [hbm] * 2,
        out_specs=vmem,
        scratch_shapes=[
            pltpu.VMEM((slots, row_count), bf16),
            pltpu.VMEM((blocks, slots), bf16),
            pltpu.VMEM((slots, blocks), bf16),
            pltpu.VMEM((row_count, slots), bf16),
            travel,
            travel,
            travel,
            travel,
            pltpu.VMEM((comps, blocks, nodes), f32),
            pltpu.VMEM((comps, half, nodes), f32),
            pltpu.VMEM((comps, half, nodes), f32),
            pltpu.VMEM((comps, blocks, nodes), f32),
            pltpu.VMEM((half, nodes, nodes), bf16),
            pltpu.VMEM((half, nodes, nodes), bf16),
            pltpu.SemaphoreType.DMA((2,)),
            pltpu.SemaphoreType.DMA((2, comps)),
            pltpu.SemaphoreType.DMA((2, comps)),
            pltpu.SemaphoreType.DMA((2, comps)),
            pltpu.SemaphoreType.DMA((2, comps)),
        ],
        compiler_params=pltpu.CompilerParams(
            collective_id=0, has_side_effects=True, vmem_limit_bytes=48 * 1024 * 1024
        ),
    )(
        contributions,
        send.reshape(slots, 1),
        jnp.broadcast_to(send.reshape(1, slots), (SUBLANES, slots)),
        arrival.reshape(slots, 1),
        jnp.broadcast_to(arrival.reshape(1, slots), (SUBLANES, slots)),
        dual_diagonal,
        mortar,
        master_inverse,
    )


def solution(mesh):
    placed = (
        P("narrow", None, "wide", None),
        P("wide", None),
        P("wide", None),
        P("wide", None),
        P("wide", None, None),
        P("wide", None, None),
    )
    return jax.shard_map(
        shards,
        mesh=mesh,
        in_specs=placed,
        out_specs=P("narrow", None, "wide", None),
        check_vma=False,
    )
```

profile of v0, /device:TPU:0, one launch (start us, length us, event | category | flops | bytes accessed | tf_op | source)
XLA Modules:
  0.0 70.8 jit_solution(6477542949376583943)
XLA Ops:
  0.0 0.7 reduce
  0.7 0.1 reshape.16
  0.8 0.1 broadcast_in_dim.14
  0.9 0.7 reduce.1
  1.6 0.1 reshape.18
  1.7 0.1 broadcast_in_dim.16
  1.8 0.2 reshape.21.arrival_col
  2.0 0.2 reshape.20.send_col
  2.2 0.0 copy-start
  2.2 1.1 %copy-done = f32[1,3,512,128]{3,2,1,0:T(8,128)S(1)} copy-done((f32[1,3,512,128]{3,2,1,0:T(8,128)S(1)}, f32[1,3,512,128]{3,2,1,0:T(8,128)}, u32[]{:S(2)}) %copy-start) | copy-done | bytes 786456
  3.3 0.0 copy-start.1
  3.3 0.9 %copy-done.1 = f32[256,128]{1,0:T(8,128)S(1)} copy-done((f32[256,128]{1,0:T(8,128)S(1)}, f32[256,128]{1,0:T(8,128)}, u32[]{:S(2)}) %copy-start.1) | copy-done | bytes 131096
  4.2 65.7 %shard_map.64 = f32[1,3,512,128]{3,2,1,0:T(8,128)S(1)} custom-call(f32[1,3,512,128]{3,2,1,0:T(8,128)S(1)} %copy-done, s32[896,1]{1,0:T(8,128)S(1)} %reshape.20.send_col, s32[8,896]{1,0:T(8,128)S(1)} %broadcast_in_dim.15.send_row, s32[896,1]{1,0:T(8,128)S(1)} %reshape.21.arrival_col, s32[8,896]{1,0:T(8,128)S(1)} %broadcast_in_dim.17.arrival_row, ...), custom_call_target="tpu_custom_call" | custom-call | tf_op jit(solution)/shard_map/pallas_call | solution.py:233
  69.9 0.9 %copy.10 = f32[1,3,512,128]{3,2,1,0:T(8,128)} copy(f32[1,3,512,128]{3,2,1,0:T(8,128)S(1)} %shard_map.64) | data formatting | bytes 1572864
  (4 shorter events, 0.0 us)
Async XLA Ops:
  2.2 1.1 %copy-start = (f32[1,3,512,128]{3,2,1,0:T(8,128)S(1)}, f32[1,3,512,128]{3,2,1,0:T(8,128)}, u32[]{:S(2)}) copy-start(f32[1,3,512,128]{3,2,1,0:T(8,128)} %contributions.1) | copy-start | bytes 2359300
  3.3 0.9 %copy-start.1 = (f32[256,128]{1,0:T(8,128)S(1)}, f32[256,128]{1,0:T(8,128)}, u32[]{:S(2)}) copy-start(f32[256,128]{1,0:T(8,128)} %diagonal.1) | copy-start | bytes 393220
where the time goes:
time: 71 us; the launch traced here: 70.8 us
  Pallas kernels  65.7 us (93%)
  local copies, waits for them, and re-layouts  3.61 us (5%)
  other arithmetic  1.4 us (2%)
    pallas_call x1, Pallas kernels, shards(): pl.pallas_call(functools.partial(kernel, n, cap), out_shape=jax.ShapeDtyp...  65.7 us
    unnamed x5, local copies, waits for them, and re-layouts  2.91 us

commit v1 on v0

v1 whole, which is shorter than its diff:
```python
import functools

import jax
import jax.numpy as jnp
from jax import lax
from jax.experimental import pallas as pl
from jax.experimental.pallas import tpu as pltpu
from jax.sharding import PartitionSpec as P

GROUP = 16
SUBLANES = 8
LANES = 128
PLANES = 4
MESH = pl.DeviceIdType.MESH


def one_hot_dot(mask, values):
    high = values.astype(jnp.bfloat16)
    low = (values - high.astype(jnp.float32)).astype(jnp.bfloat16)
    return jnp.dot(mask, high, preferred_element_type=jnp.float32) + jnp.dot(
        mask, low, preferred_element_type=jnp.float32
    )


def block_products(vectors, matrices, transposed):
    rows = lax.broadcasted_iota(jnp.int32, vectors.shape, 0)
    total = jnp.zeros(vectors.shape, jnp.float32)
    for b in range(vectors.shape[0]):
        product = lax.dot_general(
            vectors,
            matrices(b),
            (((1,), (1 if transposed else 0,)), ((), ())),
            preferred_element_type=jnp.float32,
        )
        total = jnp.where(rows == b, product, total)
    return total


def kernel(
    n,
    cap,
    capp,
    contributions_hbm,
    send_hbm,
    arrival_hbm,
    diagonal_hbm,
    mortar_hbm,
    inverse_hbm,
    out,
    contributions,
    send_map,
    arrival_map,
    diagonal,
    mortar,
    inverse,
    send_row,
    own_row,
    far_row,
    hub_rows,
    pick_mask,
    place_mask,
    sum_mask,
    spread_mask,
    hub_sum_mask,
    hub_spread_mask,
    going,
    coming,
    hub_in,
    dense_out,
    dense_in,
    sums,
    pair,
    fix_pair,
    fixes,
    returning,
    up_in,
    relay,
    returned,
    load_sem,
    map_sem,
    fetch_sem,
    ids_send,
    ids_recv,
    own_send,
    own_recv,
    hub_send,
    hub_recv,
    dense_send,
    dense_recv,
    pair_send,
    pair_recv,
    back_send,
    back_recv,
    up_send,
    up_recv,
    ret_send,
    relay_send,
    ret_recv,
):
    me = lax.axis_index("wide")
    side = lax.axis_index("narrow")
    comps, row_count, nodes = out.shape[1:]
    m = n // 2
    p = n // PLANES
    slots = m * capp
    blocks = sums.shape[1]
    half = blocks // 2
    upper = me // m
    local = lax.rem(me, m)
    line = lax.rem(me, p)
    base = upper * m
    far_base = (1 - upper) * m
    my_hubs = (1 + upper) * p
    far_hub = (2 - upper) * p + line
    is_hub = me // p == 1 + upper
    is_outer = jnp.logical_not(is_hub)
    my_plane = local // p
    far_planes = (1 - upper, upper)
    mine = pl.multiple_of(side * half, half)
    theirs = pl.multiple_of((1 - side) * half, half)

    if capp > cap:
        first_pad = cap // SUBLANES * SUBLANES
        pad = pl.ds(first_pad, capp - first_pad)
        empty = jnp.zeros((comps, m, capp - first_pad, nodes), jnp.float32)
        coming[:, :, pad, :] = empty
        hub_in[:, 0, :, pad, :] = empty
        hub_in[:, 1, :, pad, :] = empty
        returned[:, 0:m, pad, :] = empty
        returned[:, m:n, pad, :] = empty

    barrier = pltpu.get_barrier_semaphore()

    def greet(device):
        pl.semaphore_signal(barrier, inc=1, device_id=device, device_id_type=MESH)

    def greet_half(k, carry):
        greet({"wide": base + lax.rem(local + k, m)})
        return carry

    lax.fori_loop(1, m, greet_half, 0)
    greet({"narrow": 1 - side})
    for s in range(2):
        greet({"wide": far_hub, "narrow": s})

    @pl.when(is_hub)
    def _():
        for s in range(2):
            for j in range(2):
                greet({"wide": far_base + j * p + line, "narrow": s})

    map_loads = [
        pltpu.make_async_copy(send_hbm, send_map, map_sem.at[0]),
        pltpu.make_async_copy(arrival_hbm, arrival_map, map_sem.at[1]),
    ]
    loads = [
        pltpu.make_async_copy(contributions_hbm.at[0, c], contributions.at[c], load_sem.at[c])
        for c in range(comps)
    ]
    fetches = [
        pltpu.make_async_copy(diagonal_hbm.at[pl.ds(mine, half)], diagonal, fetch_sem.at[0]),
        pltpu.make_async_copy(mortar_hbm.at[pl.ds(mine, half)], mortar, fetch_sem.at[1]),
        pltpu.make_async_copy(inverse_hbm.at[pl.ds(mine, half)], inverse, fetch_sem.at[2]),
    ]
    for copy in map_loads + loads + fetches:
        copy.start()

    def stretch(target, first, source, count):
        target[...] = jnp.full(target.shape, -1, jnp.int32)
        for k in range(count):
            ids = source[0:1, (first + k) * cap : (first + k + 1) * cap]
            target[:, k * capp : k * capp + cap] = jnp.broadcast_to(ids, (SUBLANES, cap))

    def row_mask(ids, count):
        shape = (count // SUBLANES, SUBLANES, ids.shape[1])
        rows = lax.broadcasted_iota(jnp.int32, shape, 0) * SUBLANES + lax.broadcasted_iota(
            jnp.int32, shape, 1
        )
        hits = jnp.where(ids[None] == rows, 1.0, 0.0)
        return hits.reshape(count, ids.shape[1]).astype(jnp.bfloat16)

    def column_mask(target, ids):
        lanes = lax.broadcasted_iota(jnp.int32, (LANES, LANES), 1)
        for k in range(target.shape[0] // LANES):
            row = ids[0:1, k * LANES : (k + 1) * LANES]
            column = jnp.broadcast_to(row, (LANES, LANES)).T
            for g in range(target.shape[1] // LANES):
                hits = jnp.where(column == lanes + g * LANES, 1.0, 0.0)
                target[k * LANES : (k + 1) * LANES, g * LANES : (g + 1) * LANES] = hits.astype(
                    jnp.bfloat16
                )

    def wait_bytes(view, sem):
        pltpu.make_async_copy(view, view, sem).wait()

    def remote(source, target, send_sem, recv_sem, device):
        return pltpu.make_async_remote_copy(
            src_ref=source,
            dst_ref=target,
            send_sem=send_sem,
            recv_sem=recv_sem,
            device_id=device,
            device_id_type=MESH,
        )

    live = pl.ds(0, cap)

    def pick(c):
        loads[c].wait()
        going[c] = one_hot_dot(pick_mask[...], contributions[c]).reshape(n, capp, nodes)

    def send_hub(c):
        for j in far_planes:

            def to_hub(k, carry):
                other = lax.rem(line + k, p)
                remote(
                    going.at[c, far_base + j * p + other, live],
                    hub_in.at[c, j, local, live],
                    hub_send.at[c],
                    hub_recv.at[c, j],
                    {"wide": my_hubs + other},
                ).start()
                return carry

            @pl.when(is_outer)
            def _():
                to_hub(0, 0)

            lax.fori_loop(1, p, to_hub, 0)

        @pl.when(is_hub)
        def _():
            for j in range(2):
                hub_in[c, j, local] = going[c, far_base + j * p + line]

    def send_own(c):
        def to_owner(k, carry):
            peer = base + lax.rem(local + k, m)
            remote(
                going.at[c, peer, live],
                coming.at[c, local, live],
                own_send.at[c],
                own_recv.at[c],
                {"wide": peer},
            ).start()
            return carry

        lax.fori_loop(1, m, to_owner, 0)
        coming[c, local] = going[c, me]

    def gather_hub(c):
        @pl.when(is_hub)
        def _():
            for j in far_planes:
                wait_bytes(hub_in.at[c, j, pl.ds(0, m - 1), live], hub_recv.at[c, j])
                dense_out[c, j] = one_hot_dot(
                    hub_sum_mask[j], hub_in[c, j].reshape(slots, nodes)
                )
                for s in range(2):
                    remote(
                        dense_out.at[c, j, pl.ds(s * half, half)],
                        dense_in.at[c, side],
                        dense_send.at[c, j],
                        dense_recv.at[c],
                        {"wide": far_base + j * p + line, "narrow": s},
                    ).start()

    def swap(c):
        return remote(
            sums.at[c, pl.ds(theirs, half)],
            pair.at[c, side],
            pair_send.at[c],
            pair_recv.at[c],
            {"narrow": 1 - side},
        )

    def gather_own(c):
        wait_bytes(coming.at[c, pl.ds(0, m - 1), live], own_recv.at[c])
        sums[c] = one_hot_dot(sum_mask[...], coming[c].reshape(slots, nodes))
        swap(c).start()
        pair[c, side] = sums[c, pl.ds(mine, half), :]

    def swap_back(c):
        return remote(
            fix_pair.at[c, 1 - side],
            fixes.at[c, pl.ds(mine, half)],
            back_send.at[c],
            back_recv.at[c],
            {"narrow": 1 - side},
        )

    def solve(c):
        swap(c).wait()
        wait_bytes(dense_in.at[c], dense_recv.at[c])

        def condense(g, carry):
            first = pl.multiple_of(g * GROUP, GROUP)
            rows = pl.ds(first, GROUP)
            slave = pair[c, 0, rows, :] + dense_in[c, 0, rows, :]
            master = pair[c, 1, rows, :] + dense_in[c, 1, rows, :]
            scale = diagonal[rows, :]
            low = (slave / scale).astype(jnp.bfloat16)
            condensed = master + block_products(low, lambda b: mortar[first + b], False)
            master_fix = block_products(
                condensed.astype(jnp.bfloat16), lambda b: inverse[first + b], True
            )
            slave_fix = (
                block_products(master_fix.astype(jnp.bfloat16), lambda b: mortar[first + b], True)
                / scale
            )
            fix_pair[c, 0, rows, :] = slave_fix
            fix_pair[c, 1, rows, :] = master_fix
            return carry

        lax.fori_loop(0, half // GROUP, condense, 0, unroll=2)
        swap_back(c).start()
        for s in range(2):
            remote(
                fix_pair.at[c, s],
                up_in.at[c, my_plane, pl.ds(mine, half)],
                up_send.at[c],
                up_recv.at[c, my_plane],
                {"wide": far_hub, "narrow": s},
            ).start()
        fixes[c, pl.ds(mine, half), :] = fix_pair[c, side]

    def return_own(c):
        swap_back(c).wait()
        returning[c] = one_hot_dot(spread_mask[...], fixes[c]).reshape(m, capp, nodes)

        def to_source(k, carry):
            peer = lax.rem(local + k, m)
            remote(
                returning.at[c, peer, live],
                returned.at[c, me, live],
                ret_send.at[c],
                ret_recv.at[c],
                {"wide": base + peer},
            ).start()
            return carry

        lax.fori_loop(1, m, to_source, 0)
        returned[c, me] = returning[c, local]

    def return_hub(c):
        @pl.when(is_hub)
        def _():
            for j in far_planes:
                owner = far_base + j * p + line
                wait_bytes(up_in.at[c, j], up_recv.at[c, j])
                relay[c, j] = one_hot_dot(hub_spread_mask[j], up_in[c, j]).reshape(m, capp, nodes)

                def to_source(k, carry):
                    peer = lax.rem(local + k, m)
                    remote(
                        relay.at[c, j, peer, live],
                        returned.at[c, owner, live],
                        relay_send.at[c, j],
                        ret_recv.at[c],
                        {"wide": base + peer},
                    ).start()
                    return carry

                lax.fori_loop(1, m, to_source, 0)
                returned[c, owner] = relay[c, j, local]

    def place(c):
        @pl.when(is_hub)
        def _():
            wait_bytes(returned.at[c, pl.ds(0, n - 3), live], ret_recv.at[c])

        @pl.when(is_outer)
        def _():
            wait_bytes(returned.at[c, pl.ds(0, n - 1), live], ret_recv.at[c])

        out[0, c] = one_hot_dot(place_mask[...], returned[c].reshape(n * capp, nodes))

    map_loads[0].wait()
    stretch(send_row, 0, send_map, n)
    column_mask(pick_mask, send_row)
    map_loads[1].wait()

    @pl.when(upper == 0)
    def _():
        stretch(own_row, 0, arrival_map, m)
        stretch(far_row, m, arrival_map, m)

    @pl.when(upper == 1)
    def _():
        stretch(far_row, 0, arrival_map, m)
        stretch(own_row, m, arrival_map, m)

    pick(0)
    pl.semaphore_wait(barrier, jnp.where(is_hub, m + 6, m + 2))
    send_ids = remote(
        far_row,
        hub_rows.at[my_plane],
        ids_send.at[0],
        ids_recv.at[my_plane],
        {"wide": far_hub},
    )
    send_ids.start()
    send_hub(0)
    send_own(0)
    for c in range(1, comps):
        pick(c)
        send_hub(c)
        send_own(c)

    @pl.when(is_hub)
    def _():
        for j in far_planes:
            wait_bytes(hub_rows.at[j], ids_recv.at[j])
            hub_sum_mask[j] = row_mask(hub_rows[j], blocks)

    gather_hub(0)
    sum_mask[...] = row_mask(own_row[...], blocks)
    column_mask(spread_mask, own_row)
    gather_own(0)
    for fetch in fetches:
        fetch.wait()
    place_mask[...] = row_mask(send_row[...], row_count)
    gather_hub(1)
    solve(0)
    gather_own(1)
    return_own(0)

    @pl.when(is_hub)
    def _():
        for j in range(2):
            column_mask(hub_spread_mask.at[j], hub_rows.at[j])

    gather_hub(2)
    return_hub(0)
    solve(1)
    gather_own(2)
    return_own(1)
    solve(2)
    return_hub(1)
    return_own(2)
    place(0)
    return_hub(2)
    place(1)
    place(2)

    send_ids.wait_send()
    for c in range(comps):
        wait_bytes(going.at[c, pl.ds(0, m - 1), live], own_send.at[c])
        wait_bytes(returning.at[c, pl.ds(0, m - 1), live], ret_send.at[c])
        wait_bytes(fix_pair.at[c], up_send.at[c])

        @pl.when(is_hub)
        def _():
            wait_bytes(going.at[c, pl.ds(0, m - 2), live], hub_send.at[c])
            for j in range(2):
                wait_bytes(dense_out.at[c, j], dense_send.at[c, j])
                wait_bytes(relay.at[c, j, pl.ds(0, m - 1), live], relay_send.at[c, j])

        @pl.when(is_outer)
        def _():
            wait_bytes(going.at[c, pl.ds(0, m), live], hub_send.at[c])


def shards(contributions, send_map, arrival_map, dual_diagonal, mortar, master_inverse):
    n = lax.axis_size("wide")
    _, comps, row_count, nodes = contributions.shape
    blocks = dual_diagonal.shape[0]
    half = blocks // lax.axis_size("narrow")
    m = n // 2
    cap = send_map.shape[1] // n
    capp = -(-cap // SUBLANES) * SUBLANES
    while m * capp % LANES:
        capp += SUBLANES
    slots = m * capp

    f32, bf16, i32 = jnp.float32, jnp.bfloat16, jnp.int32
    dma = pltpu.SemaphoreType.DMA
    return pl.pallas_call(
        functools.partial(kernel, n, cap, capp),
        out_shape=jax.ShapeDtypeStruct((1, comps, row_count, nodes), f32),
        in_specs=[pl.BlockSpec(memory_space=pl.ANY)] * 6,
        out_specs=pl.BlockSpec(memory_space=pltpu.VMEM),
        scratch_shapes=[
            pltpu.VMEM((comps, row_count, nodes), f32),
            pltpu.VMEM((1, n * cap), i32),
            pltpu.VMEM((1, n * cap), i32),
            pltpu.VMEM((half, nodes), f32),
            pltpu.VMEM((half, nodes, nodes), bf16),
            pltpu.VMEM((half, nodes, nodes), bf16),
            pltpu.VMEM((SUBLANES, n * capp), i32),
            pltpu.VMEM((SUBLANES, slots), i32),
            pltpu.VMEM((SUBLANES, slots), i32),
            pltpu.VMEM((2, SUBLANES, slots), i32),
            pltpu.VMEM((n * capp, row_count), bf16),
            pltpu.VMEM((row_count, n * capp), bf16),
            pltpu.VMEM((blocks, slots), bf16),
            pltpu.VMEM((slots, blocks), bf16),
            pltpu.VMEM((2, blocks, slots), bf16),
            pltpu.VMEM((2, slots, blocks), bf16),
            pltpu.VMEM((comps, n, capp, nodes), f32),
            pltpu.VMEM((comps, m, capp, nodes), f32),
            pltpu.VMEM((comps, 2, m, capp, nodes), f32),
            pltpu.VMEM((comps, 2, blocks, nodes), f32),
            pltpu.VMEM((comps, 2, half, nodes), f32),
            pltpu.VMEM((comps, blocks, nodes), f32),
            pltpu.VMEM((comps, 2, half, nodes), f32),
            pltpu.VMEM((comps, 2, half, nodes), f32),
            pltpu.VMEM((comps, blocks, nodes), f32),
            pltpu.VMEM((comps, m, capp, nodes), f32),
            pltpu.VMEM((comps, 2, blocks, nodes), f32),
            pltpu.VMEM((comps, 2, m, capp, nodes), f32),
            pltpu.VMEM((comps, n, capp, nodes), f32),
            dma((comps,)),
            dma((2,)),
            dma((3,)),
            dma((1,)),
            dma((2,)),
            dma((comps,)),
            dma((comps,)),
            dma((comps,)),
            dma((comps, 2)),
            dma((comps, 2)),
            dma((comps,)),
            dma((comps,)),
            dma((comps,)),
            dma((comps,)),
            dma((comps,)),
            dma((comps,)),
            dma((comps, 2)),
            dma((comps,)),
            dma((comps, 2)),
            dma((comps,)),
        ],
        compiler_params=pltpu.CompilerParams(
            collective_id=0, has_side_effects=True, vmem_limit_bytes=48 * 1024 * 1024
        ),
    )(contributions, send_map, arrival_map, dual_diagonal, mortar, master_inverse)


def solution(mesh):
    placed = (
        P("narrow", None, "wide", None),
        P("wide", None),
        P("wide", None),
        P("wide", None),
        P("wide", None, None),
        P("wide", None, None),
    )
    return jax.shard_map(
        shards,
        mesh=mesh,
        in_specs=placed,
        out_specs=P("narrow", None, "wide", None),
        check_vma=False,
    )
```

time: 71 us -> 69.7 us (0.982)
  other arithmetic: 1.4 us -> 0 us
    unnamed x2 -> x0, other arithmetic: 1.4 us -> none
    unnamed x5 -> x9, local copies, waits for them, and re-layouts: 2.91 us -> 4.29 us
where the time goes in v1:
time: 69.7 us; the launch traced here: 69.5 us
  Pallas kernels  65.2 us (94%)
  local copies, waits for them, and re-layouts  4.29 us (6%)
    pallas_call x1, Pallas kernels, shards(): pl.pallas_call(functools.partial(kernel, n, cap, capp), out_shape=jax.Sha...  65.2 us
    unnamed x9, local copies, waits for them, and re-layouts  4.29 us

profile of v1, /device:TPU:0, one launch (start us, length us, event | category | flops | bytes accessed | tf_op | source)
XLA Modules:
  0.0 69.5 jit_solution(14950054684078983686)
XLA Ops:
  0.0 0.0 copy-start
  0.0 1.1 %copy-done = f32[1,3,512,128]{3,2,1,0:T(8,128)S(1)} copy-done((f32[1,3,512,128]{3,2,1,0:T(8,128)S(1)}, f32[1,3,512,128]{3,2,1,0:T(8,128)}, u32[]{:S(2)}) %copy-start) | copy-done | bytes 786456
  1.1 0.0 copy-start.1
  1.1 0.9 %copy-done.1 = f32[256,128]{1,0:T(8,128)S(1)} copy-done((f32[256,128]{1,0:T(8,128)S(1)}, f32[256,128]{1,0:T(8,128)}, u32[]{:S(2)}) %copy-start.1) | copy-done | bytes 131096
  2.0 0.0 copy-start.2
  2.0 0.7 copy-done.2
  2.7 0.0 copy-start.3
  2.7 0.7 copy-done.3
  3.4 65.2 %shard_map.64 = f32[1,3,512,128]{3,2,1,0:T(8,128)S(1)} custom-call(f32[1,3,512,128]{3,2,1,0:T(8,128)S(1)} %copy-done, s32[1,800]{1,0:T(1,128)S(1)} %copy-done.2, s32[1,800]{1,0:T(1,128)S(1)} %copy-done.3, f32[256,128]{1,0:T(8,128)S(1)} %copy-done.1, bf16[256,128,128]{2,1,0:T(8,128)(2,1)} %mortar_hbm.1, bf16[256,128,128]{2,1,0:T(8,128)(2,1)} %inverse_hbm.1), custom_call_target="tpu_custom_call" | custom-call | tf_op jit(solution)/shard_map/pallas_call | solution.py:479
  68.6 0.9 %copy.8 = f32[1,3,512,128]{3,2,1,0:T(8,128)} copy(f32[1,3,512,128]{3,2,1,0:T(8,128)S(1)} %shard_map.64) | data formatting | bytes 1572864
Async XLA Ops:
  0.0 1.1 %copy-start = (f32[1,3,512,128]{3,2,1,0:T(8,128)S(1)}, f32[1,3,512,128]{3,2,1,0:T(8,128)}, u32[]{:S(2)}) copy-start(f32[1,3,512,128]{3,2,1,0:T(8,128)} %contributions_hbm.1) | copy-start | bytes 2359300
  1.1 0.9 %copy-start.1 = (f32[256,128]{1,0:T(8,128)S(1)}, f32[256,128]{1,0:T(8,128)}, u32[]{:S(2)}) copy-start(f32[256,128]{1,0:T(8,128)} %diagonal_hbm.1) | copy-start | bytes 393220
  2.0 0.7 copy-start.2
  2.7 0.7 copy-start.3

commit v2 on v1

v2 whole, which is shorter than its diff:
```python
import functools

import jax
import jax.numpy as jnp
from jax import lax
from jax.experimental import pallas as pl
from jax.experimental.pallas import tpu as pltpu
from jax.sharding import PartitionSpec as P

GROUP = 32
SUBLANES = 8
LANES = 128
PLANES = 4
MESH = pl.DeviceIdType.MESH


def one_hot_dot(mask, values):
    nodes = values.shape[1]
    high = values.astype(jnp.bfloat16)
    low = (values - high.astype(jnp.float32)).astype(jnp.bfloat16)
    both = jnp.dot(mask, jnp.concatenate([high, low], axis=1), preferred_element_type=jnp.float32)
    return both[:, :nodes] + both[:, nodes:]


def block_products(vectors, matrices, transposed):
    nodes = vectors.shape[1]
    rows = lax.broadcasted_iota(jnp.int32, vectors.shape, 0)
    odd = lax.rem(rows, 2) == 1
    total = jnp.zeros(vectors.shape, jnp.float32)
    wide = jnp.concatenate(
        [jnp.where(odd, total, vectors), jnp.where(odd, vectors, total)], axis=1
    ).astype(jnp.bfloat16)
    for b in range(0, vectors.shape[0], 4):
        m0, m1, m2, m3 = (matrices(b + k) for k in range(4))
        if transposed:
            tile = [[m0, m1], [m2, m3]]
        else:
            tile = [[m0, m2], [m1, m3]]
        tile = jnp.concatenate([jnp.concatenate(part, axis=1) for part in tile], axis=0)
        product = lax.dot_general(
            wide,
            tile,
            (((1,), (1 if transposed else 0,)), ((), ())),
            preferred_element_type=jnp.float32,
        )
        first = (rows >= b) & (rows < b + 2)
        second = (rows >= b + 2) & (rows < b + 4)
        total = jnp.where(first, product[:, :nodes], jnp.where(second, product[:, nodes:], total))
    return total


def kernel(
    n,
    cap,
    capp,
    contributions_hbm,
    send_hbm,
    arrival_hbm,
    diagonal_hbm,
    mortar_hbm,
    inverse_hbm,
    out,
    contributions,
    send_map,
    arrival_map,
    diagonal,
    mortar,
    inverse,
    send_row,
    own_row,
    far_row,
    hub_rows,
    pick_mask,
    place_mask,
    sum_mask,
    spread_mask,
    far_spread_mask,
    hub_sum_mask,
    hub_spread_mask,
    going,
    coming,
    hub_in,
    dense_out,
    dense_in,
    sums,
    pair,
    fix_pair,
    fixes,
    returning,
    returning_far,
    up_in,
    relay,
    returned,
    load_sem,
    map_sem,
    fetch_sem,
    ids_send,
    ids_recv,
    own_send,
    own_recv,
    hub_send,
    hub_recv,
    dense_send,
    dense_recv,
    pair_send,
    pair_recv,
    back_send,
    back_recv,
    up_send,
    up_recv,
    ret_send,
    relay_send,
    ret_recv,
):
    me = lax.axis_index("wide")
    side = lax.axis_index("narrow")
    comps, row_count, nodes = out.shape[1:]
    m = n // 2
    p = n // PLANES
    slots = m * capp
    blocks = sums.shape[1]
    half = blocks // 2
    upper = me // m
    local = lax.rem(me, m)
    line = lax.rem(me, p)
    base = upper * m
    far_base = (1 - upper) * m
    my_hubs = (1 + upper) * p
    far_hub = (2 - upper) * p + line
    is_hub = me // p == 1 + upper
    is_outer = jnp.logical_not(is_hub)
    my_plane = local // p
    far_planes = (1 - upper, upper)
    mine = pl.multiple_of(side * half, half)
    theirs = pl.multiple_of((1 - side) * half, half)

    if capp > cap:
        first_pad = cap // SUBLANES * SUBLANES
        pad = pl.ds(first_pad, capp - first_pad)
        empty = jnp.zeros((comps, m, capp - first_pad, nodes), jnp.float32)
        coming[:, :, pad, :] = empty
        hub_in[:, 0, :, pad, :] = empty
        hub_in[:, 1, :, pad, :] = empty
        returned[:, 0:m, pad, :] = empty
        returned[:, m:n, pad, :] = empty

    barrier = pltpu.get_barrier_semaphore()

    def greet(device):
        pl.semaphore_signal(barrier, inc=1, device_id=device, device_id_type=MESH)

    def greet_half(k, carry):
        greet({"wide": base + lax.rem(local + k, m)})
        return carry

    lax.fori_loop(1, m, greet_half, 0)
    greet({"narrow": 1 - side})
    for s in range(2):
        greet({"wide": far_hub, "narrow": s})

    @pl.when(is_hub)
    def _():
        for s in range(2):
            for j in range(2):
                greet({"wide": far_base + j * p + line, "narrow": s})

    map_loads = [
        pltpu.make_async_copy(send_hbm, send_map, map_sem.at[0]),
        pltpu.make_async_copy(arrival_hbm, arrival_map, map_sem.at[1]),
    ]
    loads = [
        pltpu.make_async_copy(contributions_hbm.at[0, c], contributions.at[c], load_sem.at[c])
        for c in range(comps)
    ]
    fetches = [
        pltpu.make_async_copy(diagonal_hbm.at[pl.ds(mine, half)], diagonal, fetch_sem.at[0]),
        pltpu.make_async_copy(mortar_hbm.at[pl.ds(mine, half)], mortar, fetch_sem.at[1]),
        pltpu.make_async_copy(inverse_hbm.at[pl.ds(mine, half)], inverse, fetch_sem.at[2]),
    ]
    for copy in map_loads + loads + fetches:
        copy.start()

    def stretch(target, first, source, count):
        target[...] = jnp.full(target.shape, -1, jnp.int32)
        for k in range(count):
            ids = source[0:1, (first + k) * cap : (first + k + 1) * cap]
            target[:, k * capp : k * capp + cap] = jnp.broadcast_to(ids, (SUBLANES, cap))

    def row_mask(ids, count):
        shape = (count // SUBLANES, SUBLANES, ids.shape[1])
        rows = lax.broadcasted_iota(jnp.int32, shape, 0) * SUBLANES + lax.broadcasted_iota(
            jnp.int32, shape, 1
        )
        hits = jnp.where(ids[None] == rows, 1.0, 0.0)
        return hits.reshape(count, ids.shape[1]).astype(jnp.bfloat16)

    def column_mask(target, ids):
        lanes = lax.broadcasted_iota(jnp.int32, (LANES, LANES), 1)
        for k in range(target.shape[0] // LANES):
            row = ids[0:1, k * LANES : (k + 1) * LANES]
            column = jnp.broadcast_to(row, (LANES, LANES)).T
            for g in range(target.shape[1] // LANES):
                hits = jnp.where(column == lanes + g * LANES, 1.0, 0.0)
                target[k * LANES : (k + 1) * LANES, g * LANES : (g + 1) * LANES] = hits.astype(
                    jnp.bfloat16
                )

    def wait_bytes(view, sem):
        with jax.named_scope("wait"):
            pltpu.make_async_copy(view, view, sem).wait()

    def remote(source, target, send_sem, recv_sem, device):
        return pltpu.make_async_remote_copy(
            src_ref=source,
            dst_ref=target,
            send_sem=send_sem,
            recv_sem=recv_sem,
            device_id=device,
            device_id_type=MESH,
        )

    live = pl.ds(0, cap)
    straight = (comps - 1,)

    def each_peer(send):
        def cross(k, carry):
            send((1 - my_plane) * p + lax.rem(line + k, p))
            return carry

        def along(k, carry):
            send(my_plane * p + lax.rem(line + k, p))
            return carry

        lax.fori_loop(0, p, cross, 0)
        lax.fori_loop(1, p, along, 0)

    def pick(c):
        with jax.named_scope(f"pick{c}"):
            loads[c].wait()
            going[c] = one_hot_dot(pick_mask[...], contributions[c]).reshape(n, capp, nodes)

    def send_hub(c):
        with jax.named_scope(f"send_hub{c}"):
            for j in far_planes:

                def to_hub(k, carry):
                    other = lax.rem(line + k, p)
                    remote(
                        going.at[c, far_base + j * p + other, live],
                        hub_in.at[c, j, local, live],
                        hub_send.at[c],
                        hub_recv.at[c, j],
                        {"wide": my_hubs + other},
                    ).start()
                    return carry

                @pl.when(is_outer)
                def _():
                    to_hub(0, 0)

                lax.fori_loop(1, p, to_hub, 0)

            @pl.when(is_hub)
            def _():
                for j in range(2):
                    hub_in[c, j, local] = going[c, far_base + j * p + line]

    def send_own(c):
        with jax.named_scope(f"send_own{c}"):

            def to_owner(peer):
                remote(
                    going.at[c, base + peer, live],
                    coming.at[c, local, live],
                    own_send.at[c],
                    own_recv.at[c],
                    {"wide": base + peer},
                ).start()

            each_peer(to_owner)
            coming[c, local] = going[c, me]

    def gather_hub(c):
        with jax.named_scope(f"gather_hub{c}"):
            @pl.when(is_hub)
            def _():
                for j in far_planes:
                    wait_bytes(hub_in.at[c, j, pl.ds(0, m - 1), live], hub_recv.at[c, j])
                    dense_out[c, j] = one_hot_dot(
                        hub_sum_mask[j], hub_in[c, j].reshape(slots, nodes)
                    )
                    for s in range(2):
                        remote(
                            dense_out.at[c, j, pl.ds(s * half, half)],
                            dense_in.at[c, side],
                            dense_send.at[c, j],
                            dense_recv.at[c],
                            {"wide": far_base + j * p + line, "narrow": s},
                        ).start()

    def swap(c):
        return remote(
            sums.at[c, pl.ds(theirs, half)],
            pair.at[c, side],
            pair_send.at[c],
            pair_recv.at[c],
            {"narrow": 1 - side},
        )

    def gather_own(c):
        with jax.named_scope(f"gather_own{c}"):
            wait_bytes(coming.at[c, pl.ds(0, m - 1), live], own_recv.at[c])
            sums[c] = one_hot_dot(sum_mask[...], coming[c].reshape(slots, nodes))
            swap(c).start()
            pair[c, side] = sums[c, pl.ds(mine, half), :]

    def swap_back(c):
        return remote(
            fix_pair.at[c, 1 - side],
            fixes.at[c, pl.ds(mine, half)],
            back_send.at[c],
            back_recv.at[c],
            {"narrow": 1 - side},
        )

    def solve(c):
        with jax.named_scope(f"solve{c}"):
            with jax.named_scope("wait_swap"):
                swap(c).wait()
            wait_bytes(dense_in.at[c], dense_recv.at[c])

            def condense(g, carry):
                first = pl.multiple_of(g * GROUP, GROUP)
                rows = pl.ds(first, GROUP)
                slave = pair[c, 0, rows, :] + dense_in[c, 0, rows, :]
                master = pair[c, 1, rows, :] + dense_in[c, 1, rows, :]
                scale = diagonal[rows, :]
                condensed = master + block_products(slave / scale, lambda b: mortar[first + b], False)
                master_fix = block_products(condensed, lambda b: inverse[first + b], True)
                slave_fix = block_products(master_fix, lambda b: mortar[first + b], True) / scale
                fix_pair[c, 0, rows, :] = slave_fix
                fix_pair[c, 1, rows, :] = master_fix
                return carry

            lax.fori_loop(0, half // GROUP, condense, 0, unroll=2)
            swap_back(c).start()
            if c not in straight:
                for s in range(2):
                    remote(
                        fix_pair.at[c, s],
                        up_in.at[c, my_plane, pl.ds(mine, half)],
                        up_send.at[c],
                        up_recv.at[c, my_plane],
                        {"wide": far_hub, "narrow": s},
                    ).start()
            fixes[c, pl.ds(mine, half), :] = fix_pair[c, side]

    def return_own(c):
        with jax.named_scope(f"return_own{c}"):
            with jax.named_scope("wait_back"):
                swap_back(c).wait()
            if c in straight:
                returning_far[c] = one_hot_dot(far_spread_mask[...], fixes[c]).reshape(
                    m, capp, nodes
                )

                def to_far(k, carry):
                    peer = lax.rem(local + k, m)
                    remote(
                        returning_far.at[c, peer, live],
                        returned.at[c, me, live],
                        ret_send.at[c],
                        ret_recv.at[c],
                        {"wide": far_base + peer},
                    ).start()
                    return carry

                lax.fori_loop(0, m, to_far, 0)
            returning[c] = one_hot_dot(spread_mask[...], fixes[c]).reshape(m, capp, nodes)

            def to_source(peer):
                remote(
                    returning.at[c, peer, live],
                    returned.at[c, me, live],
                    ret_send.at[c],
                    ret_recv.at[c],
                    {"wide": base + peer},
                ).start()

            each_peer(to_source)
            returned[c, me] = returning[c, local]

    def return_hub(c):
        @pl.when(is_hub)
        def _():
            with jax.named_scope(f"return_hub{c}"):
                for j in far_planes:
                    owner = far_base + j * p + line
                    wait_bytes(up_in.at[c, j], up_recv.at[c, j])
                    relay[c, j] = one_hot_dot(hub_spread_mask[j], up_in[c, j]).reshape(
                        m, capp, nodes
                    )

                    def to_source(peer):
                        remote(
                            relay.at[c, j, peer, live],
                            returned.at[c, owner, live],
                            relay_send.at[c, j],
                            ret_recv.at[c],
                            {"wide": base + peer},
                        ).start()

                    each_peer(to_source)
                    returned[c, owner] = relay[c, j, local]

    def place(c):
        with jax.named_scope(f"place{c}"):
            if c in straight:
                wait_bytes(returned.at[c, pl.ds(0, n - 1), live], ret_recv.at[c])
            else:

                @pl.when(is_hub)
                def _():
                    wait_bytes(returned.at[c, pl.ds(0, n - 3), live], ret_recv.at[c])

                @pl.when(is_outer)
                def _():
                    wait_bytes(returned.at[c, pl.ds(0, n - 1), live], ret_recv.at[c])

            out[0, c] = one_hot_dot(place_mask[...], returned[c].reshape(n * capp, nodes))

    map_loads[0].wait()
    with jax.named_scope("pick_mask"):
        stretch(send_row, 0, send_map, n)
        column_mask(pick_mask, send_row)
    map_loads[1].wait()

    @pl.when(upper == 0)
    def _():
        stretch(own_row, 0, arrival_map, m)
        stretch(far_row, m, arrival_map, m)

    @pl.when(upper == 1)
    def _():
        stretch(far_row, 0, arrival_map, m)
        stretch(own_row, m, arrival_map, m)

    pick(0)
    with jax.named_scope("entry"):
        pl.semaphore_wait(barrier, jnp.where(is_hub, m + 6, m + 2))
    send_ids = remote(
        far_row,
        hub_rows.at[my_plane],
        ids_send.at[0],
        ids_recv.at[my_plane],
        {"wide": far_hub},
    )
    send_ids.start()
    send_hub(0)
    for c in range(1, comps):
        pick(c)
        send_hub(c)
        send_own(c - 1)
    send_own(comps - 1)

    @pl.when(is_hub)
    def _():
        with jax.named_scope("hub_sum_mask"):
            for j in far_planes:
                wait_bytes(hub_rows.at[j], ids_recv.at[j])
                hub_sum_mask[j] = row_mask(hub_rows[j], blocks)

    gather_hub(0)
    with jax.named_scope("own_masks"):
        sum_mask[...] = row_mask(own_row[...], blocks)
        column_mask(spread_mask, own_row)
        column_mask(far_spread_mask, far_row)
    gather_own(0)
    for fetch in fetches:
        fetch.wait()
    with jax.named_scope("place_mask"):
        place_mask[...] = row_mask(send_row[...], row_count)
    gather_hub(1)
    solve(0)
    gather_own(1)
    return_own(0)

    @pl.when(is_hub)
    def _():
        with jax.named_scope("hub_spread_mask"):
            for j in range(2):
                column_mask(hub_spread_mask.at[j], hub_rows.at[j])

    gather_hub(2)
    solve(1)
    gather_own(2)
    return_hub(0)
    return_own(1)
    return_hub(1)
    solve(2)
    return_own(2)
    place(0)
    place(1)
    place(2)

    with jax.named_scope("drain"):
        send_ids.wait_send()
        for c in range(comps):
            wait_bytes(going.at[c, pl.ds(0, m - 1), live], own_send.at[c])
            if c in straight:
                wait_bytes(going.at[c, pl.ds(0, n - 1), live], ret_send.at[c])
            else:
                wait_bytes(returning.at[c, pl.ds(0, m - 1), live], ret_send.at[c])
                wait_bytes(fix_pair.at[c], up_send.at[c])

            @pl.when(is_hub)
            def _():
                wait_bytes(going.at[c, pl.ds(0, m - 2), live], hub_send.at[c])
                for j in range(2):
                    wait_bytes(dense_out.at[c, j], dense_send.at[c, j])
                    if c not in straight:
                        wait_bytes(relay.at[c, j, pl.ds(0, m - 1), live], relay_send.at[c, j])

            @pl.when(is_outer)
            def _():
                wait_bytes(going.at[c, pl.ds(0, m), live], hub_send.at[c])


def shards(contributions, send_map, arrival_map, dual_diagonal, mortar, master_inverse):
    n = lax.axis_size("wide")
    _, comps, row_count, nodes = contributions.shape
    blocks = dual_diagonal.shape[0]
    half = blocks // lax.axis_size("narrow")
    m = n // 2
    cap = send_map.shape[1] // n
    capp = -(-cap // SUBLANES) * SUBLANES
    while m * capp % LANES:
        capp += SUBLANES
    slots = m * capp

    f32, bf16, i32 = jnp.float32, jnp.bfloat16, jnp.int32
    dma = pltpu.SemaphoreType.DMA
    return pl.pallas_call(
        functools.partial(kernel, n, cap, capp),
        out_shape=jax.ShapeDtypeStruct((1, comps, row_count, nodes), f32),
        in_specs=[pl.BlockSpec(memory_space=pltpu.HBM)] * 6,
        out_specs=pl.BlockSpec(memory_space=pltpu.VMEM),
        scratch_shapes=[
            pltpu.VMEM((comps, row_count, nodes), f32),
            pltpu.VMEM((1, n * cap), i32),
            pltpu.VMEM((1, n * cap), i32),
            pltpu.VMEM((half, nodes), f32),
            pltpu.VMEM((half, nodes, nodes), bf16),
            pltpu.VMEM((half, nodes, nodes), bf16),
            pltpu.VMEM((SUBLANES, n * capp), i32),
            pltpu.VMEM((SUBLANES, slots), i32),
            pltpu.VMEM((SUBLANES, slots), i32),
            pltpu.VMEM((2, SUBLANES, slots), i32),
            pltpu.VMEM((n * capp, row_count), bf16),
            pltpu.VMEM((row_count, n * capp), bf16),
            pltpu.VMEM((blocks, slots), bf16),
            pltpu.VMEM((slots, blocks), bf16),
            pltpu.VMEM((slots, blocks), bf16),
            pltpu.VMEM((2, blocks, slots), bf16),
            pltpu.VMEM((2, slots, blocks), bf16),
            pltpu.VMEM((comps, n, capp, nodes), f32),
            pltpu.VMEM((comps, m, capp, nodes), f32),
            pltpu.VMEM((comps, 2, m, capp, nodes), f32),
            pltpu.VMEM((comps, 2, blocks, nodes), f32),
            pltpu.VMEM((comps, 2, half, nodes), f32),
            pltpu.VMEM((comps, blocks, nodes), f32),
            pltpu.VMEM((comps, 2, half, nodes), f32),
            pltpu.VMEM((comps, 2, half, nodes), f32),
            pltpu.VMEM((comps, blocks, nodes), f32),
            pltpu.VMEM((comps, m, capp, nodes), f32),
            pltpu.VMEM((comps, m, capp, nodes), f32),
            pltpu.VMEM((comps, 2, blocks, nodes), f32),
            pltpu.VMEM((comps, 2, m, capp, nodes), f32),
            pltpu.VMEM((comps, n, capp, nodes), f32),
            dma((comps,)),
            dma((2,)),
            dma((3,)),
            dma((1,)),
            dma((2,)),
            dma((comps,)),
            dma((comps,)),
            dma((comps,)),
            dma((comps, 2)),
            dma((comps, 2)),
            dma((comps,)),
            dma((comps,)),
            dma((comps,)),
            dma((comps,)),
            dma((comps,)),
            dma((comps,)),
            dma((comps, 2)),
            dma((comps,)),
            dma((comps, 2)),
            dma((comps,)),
        ],
        compiler_params=pltpu.CompilerParams(
            collective_id=0, has_side_effects=True, vmem_limit_bytes=67043328
        ),
    )(contributions, send_map, arrival_map, dual_diagonal, mortar, master_inverse)


def solution(mesh):
    placed = (
        P("narrow", None, "wide", None),
        P("wide", None),
        P("wide", None),
        P("wide", None),
        P("wide", None, None),
        P("wide", None, None),
    )
    return jax.shard_map(
        shards,
        mesh=mesh,
        in_specs=placed,
        out_specs=P("narrow", None, "wide", None),
        check_vma=False,
    )
```

time: 69.7 us -> 60 us (0.86)
  Pallas kernels: 65.2 us -> 57.8 us
  local copies, waits for them, and re-layouts: 4.29 us -> 2.06 us
    pallas_call x1, Pallas kernels: 65.2 us -> 57.8 us  [shards(): pl.pallas_call(functools.partial(kernel, n, cap, capp), out_shape=jax.Sha...]
    unnamed x9 -> x1, local copies, waits for them, and re-layouts: 4.29 us -> 2.06 us
where the time goes in v2:
time: 60 us; the launch traced here: 59.9 us
  Pallas kernels  57.8 us (96%)
  local copies, waits for them, and re-layouts  2.06 us (3%)
    pallas_call x1, Pallas kernels, shards(): pl.pallas_call(functools.partial(kernel, n, cap, capp), out_shape=jax.Sha...  57.8 us
    unnamed x1, local copies, waits for them, and re-layouts  2.06 us

profile of v2, /device:TPU:0, one launch (start us, length us, event | category | flops | bytes accessed | tf_op | source)
XLA Modules:
  0.0 59.9 jit_solution(5617451688643504229)
XLA Ops:
  0.0 57.8 %shard_map.64 = f32[1,3,512,128]{3,2,1,0:T(8,128)} custom-call(f32[1,3,512,128]{3,2,1,0:T(8,128)} %contributions_hbm.1, s32[1,800]{1,0:T(1,128)} %send_hbm.1, s32[1,800]{1,0:T(1,128)} %arrival_hbm.1, f32[256,128]{1,0:T(8,128)} %diagonal_hbm.1, bf16[256,128,128]{2,1,0:T(8,128)(2,1)} %mortar_hbm.1, bf16[256,128,128]{2,1,0:T(8,128)(2,1)} %inverse_hbm.1), custom_call_target="tpu_custom_call" | custom-call | tf_op jit(solution)/shard_map/pallas_call | solution.py:543
  57.8 2.1 %copy.8 = f32[1,3,512,128]{3,2,1,0:T(8,128)} copy(f32[1,3,512,128]{3,2,1,0:T(8,128)} %shard_map.64) | data formatting | bytes 1572864

commit v3 on v2

--- a/solution.py
+++ b/solution.py
@@ -177,7 +177,7 @@
         pltpu.make_async_copy(mortar_hbm.at[pl.ds(mine, half)], mortar, fetch_sem.at[1]),
         pltpu.make_async_copy(inverse_hbm.at[pl.ds(mine, half)], inverse, fetch_sem.at[2]),
     ]
-    for copy in map_loads + loads + fetches:
+    for copy in map_loads + loads:
         copy.start()
 
     def stretch(target, first, source, count):
@@ -220,7 +220,10 @@
         )
 
     live = pl.ds(0, cap)
-    straight = (comps - 1,)
+    straight_back = tuple(range(1, comps))
+
+    def back_planes(c):
+        return far_planes[:1] if c in straight_back else far_planes
 
     def each_peer(send):
         def cross(k, carry):
@@ -344,7 +347,8 @@
 
             lax.fori_loop(0, half // GROUP, condense, 0, unroll=2)
             swap_back(c).start()
-            if c not in straight:
+
+            def to_far_hub():
                 for s in range(2):
                     remote(
                         fix_pair.at[c, s],
@@ -353,29 +357,38 @@
                         up_recv.at[c, my_plane],
                         {"wide": far_hub, "narrow": s},
                     ).start()
+
+            if c in straight_back:
+                pl.when(is_outer)(to_far_hub)
+            else:
+                to_far_hub()
             fixes[c, pl.ds(mine, half), :] = fix_pair[c, side]
 
     def return_own(c):
         with jax.named_scope(f"return_own{c}"):
             with jax.named_scope("wait_back"):
                 swap_back(c).wait()
-            if c in straight:
-                returning_far[c] = one_hot_dot(far_spread_mask[...], fixes[c]).reshape(
-                    m, capp, nodes
-                )
-
-                def to_far(k, carry):
-                    peer = lax.rem(local + k, m)
-                    remote(
-                        returning_far.at[c, peer, live],
-                        returned.at[c, me, live],
-                        ret_send.at[c],
-                        ret_recv.at[c],
-                        {"wide": far_base + peer},
-                    ).start()
-                    return carry
-
-                lax.fori_loop(0, m, to_far, 0)
+            if c in straight_back:
+
+                @pl.when(is_hub)
+                def _():
+                    returning_far[c] = one_hot_dot(far_spread_mask[...], fixes[c]).reshape(
+                        m, capp, nodes
+                    )
+
+                    def to_far(k, carry):
+                        peer = lax.rem(local + k, m)
+                        remote(
+                            returning_far.at[c, peer, live],
+                            returned.at[c, me, live],
+                            ret_send.at[c],
+                            ret_recv.at[c],
+                            {"wide": far_base + peer},
+                        ).start()
+                        return carry
+
+                    lax.fori_loop(0, m, to_far, 0)
+
             returning[c] = one_hot_dot(spread_mask[...], fixes[c]).reshape(m, capp, nodes)
 
             def to_source(peer):
@@ -394,7 +407,7 @@
         @pl.when(is_hub)
         def _():
             with jax.named_scope(f"return_hub{c}"):
-                for j in far_planes:
+                for j in back_planes(c):
                     owner = far_base + j * p + line
                     wait_bytes(up_in.at[c, j], up_recv.at[c, j])
                     relay[c, j] = one_hot_dot(hub_spread_mask[j], up_in[c, j]).reshape(
@@ -415,17 +428,15 @@
 
     def place(c):
         with jax.named_scope(f"place{c}"):
-            if c in straight:
+            at_hub = len(back_planes(c))
+
+            @pl.when(is_hub)
+            def _():
+                wait_bytes(returned.at[c, pl.ds(0, n - 1 - at_hub), live], ret_recv.at[c])
+
+            @pl.when(is_outer)
+            def _():
                 wait_bytes(returned.at[c, pl.ds(0, n - 1), live], ret_recv.at[c])
-            else:
-
-                @pl.when(is_hub)
-                def _():
-                    wait_bytes(returned.at[c, pl.ds(0, n - 3), live], ret_recv.at[c])
-
-                @pl.when(is_outer)
-                def _():
-                    wait_bytes(returned.at[c, pl.ds(0, n - 1), live], ret_recv.at[c])
 
             out[0, c] = one_hot_dot(place_mask[...], returned[c].reshape(n * capp, nodes))
 
@@ -435,17 +446,21 @@
         column_mask(pick_mask, send_row)
     map_loads[1].wait()
 
-    @pl.when(upper == 0)
-    def _():
-        stretch(own_row, 0, arrival_map, m)
-        stretch(far_row, m, arrival_map, m)
-
-    @pl.when(upper == 1)
-    def _():
-        stretch(far_row, 0, arrival_map, m)
-        stretch(own_row, m, arrival_map, m)
-
     pick(0)
+    for fetch in fetches:
+        fetch.start()
+    with jax.named_scope("rows"):
+
+        @pl.when(upper == 0)
+        def _():
+            stretch(own_row, 0, arrival_map, m)
+            stretch(far_row, m, arrival_map, m)
+
+        @pl.when(upper == 1)
+        def _():
+            stretch(far_row, 0, arrival_map, m)
+            stretch(own_row, m, arrival_map, m)
+
     with jax.named_scope("entry"):
         pl.semaphore_wait(barrier, jnp.where(is_hub, m + 6, m + 2))
     send_ids = remote(
@@ -457,41 +472,37 @@
     )
     send_ids.start()
     send_hub(0)
-    for c in range(1, comps):
-        pick(c)
-        send_hub(c)
-        send_own(c - 1)
-    send_own(comps - 1)
+    pick(1)
+    send_hub(1)
+    send_own(0)
+    pick(2)
+    send_hub(2)
+    send_own(1)
+    send_own(2)
+    with jax.named_scope("own_masks"):
+        sum_mask[...] = row_mask(own_row[...], blocks)
+        column_mask(spread_mask, own_row)
 
     @pl.when(is_hub)
     def _():
-        with jax.named_scope("hub_sum_mask"):
+        with jax.named_scope("hub_masks"):
+            column_mask(far_spread_mask, far_row)
             for j in far_planes:
                 wait_bytes(hub_rows.at[j], ids_recv.at[j])
                 hub_sum_mask[j] = row_mask(hub_rows[j], blocks)
+                column_mask(hub_spread_mask.at[j], hub_rows.at[j])
 
     gather_hub(0)
-    with jax.named_scope("own_masks"):
-        sum_mask[...] = row_mask(own_row[...], blocks)
-        column_mask(spread_mask, own_row)
-        column_mask(far_spread_mask, far_row)
+    with jax.named_scope("place_mask"):
+        place_mask[...] = row_mask(send_row[...], row_count)
+    gather_hub(1)
     gather_own(0)
     for fetch in fetches:
         fetch.wait()
-    with jax.named_scope("place_mask"):
-        place_mask[...] = row_mask(send_row[...], row_count)
-    gather_hub(1)
     solve(0)
+    gather_hub(2)
     gather_own(1)
     return_own(0)
-
-    @pl.when(is_hub)
-    def _():
-        with jax.named_scope("hub_spread_mask"):
-            for j in range(2):
-                column_mask(hub_spread_mask.at[j], hub_rows.at[j])
-
-    gather_hub(2)
     solve(1)
     gather_own(2)
     return_hub(0)
@@ -499,6 +510,7 @@
     return_hub(1)
     solve(2)
     return_own(2)
+    return_hub(2)
     place(0)
     place(1)
     place(2)
@@ -507,23 +519,25 @@
         send_ids.wait_send()
         for c in range(comps):
             wait_bytes(going.at[c, pl.ds(0, m - 1), live], own_send.at[c])
-            if c in straight:
-                wait_bytes(going.at[c, pl.ds(0, n - 1), live], ret_send.at[c])
-            else:
-                wait_bytes(returning.at[c, pl.ds(0, m - 1), live], ret_send.at[c])
-                wait_bytes(fix_pair.at[c], up_send.at[c])
 
             @pl.when(is_hub)
             def _():
                 wait_bytes(going.at[c, pl.ds(0, m - 2), live], hub_send.at[c])
                 for j in range(2):
                     wait_bytes(dense_out.at[c, j], dense_send.at[c, j])
-                    if c not in straight:
-                        wait_bytes(relay.at[c, j, pl.ds(0, m - 1), live], relay_send.at[c, j])
+                for j in back_planes(c):
+                    wait_bytes(relay.at[c, j, pl.ds(0, m - 1), live], relay_send.at[c, j])
+                if c in straight_back:
+                    wait_bytes(going.at[c, pl.ds(0, n - 1), live], ret_send.at[c])
+                else:
+                    wait_bytes(going.at[c, pl.ds(0, m - 1), live], ret_send.at[c])
+                    wait_bytes(fix_pair.at[c], up_send.at[c])
 
             @pl.when(is_outer)
             def _():
                 wait_bytes(going.at[c, pl.ds(0, m), live], hub_send.at[c])
+                wait_bytes(going.at[c, pl.ds(0, m - 1), live], ret_send.at[c])
+                wait_bytes(fix_pair.at[c], up_send.at[c])
 
 
 def shards(contributions, send_map, arrival_map, dual_diagonal, mortar, master_inverse):
@@ -538,6 +552,10 @@
         capp += SUBLANES
     slots = m * capp
 
+    operands = tuple(
+        pltpu.with_memory_space_constraint(x, pltpu.HBM)
+        for x in (contributions, send_map, arrival_map, dual_diagonal, mortar, master_inverse)
+    )
     f32, bf16, i32 = jnp.float32, jnp.bfloat16, jnp.int32
     dma = pltpu.SemaphoreType.DMA
     return pl.pallas_call(
@@ -599,9 +617,9 @@
             dma((comps,)),
         ],
         compiler_params=pltpu.CompilerParams(
-            collective_id=0, has_side_effects=True, vmem_limit_bytes=67043328
+            collective_id=0, has_side_effects=True, vmem_limit_bytes=48 * 1024 * 1024
         ),
-    )(contributions, send_map, arrival_map, dual_diagonal, mortar, master_inverse)
+    )(*operands)
 
 
 def solution(mesh):

time: 60 us -> 58 us (0.967)
  local copies, waits for them, and re-layouts: 2.06 us -> 0.88 us
  Pallas kernels: 57.8 us -> 56.9 us
    unnamed x1, local copies, waits for them, and re-layouts: 2.06 us -> 0.88 us
    pallas_call x1, Pallas kernels: 57.8 us -> 56.9 us  [shards(): pl.pallas_call(functools.partial(kernel, n, cap, capp), out_shape=jax.Sha...]
where the time goes in v3:
time: 58 us; the launch traced here: 57.8 us
  Pallas kernels  56.9 us (98%)
  local copies, waits for them, and re-layouts  0.88 us (2%)
    pallas_call x1, Pallas kernels, shards(): pl.pallas_call(functools.partial(kernel, n, cap, capp), out_shape=jax.Sha...  56.9 us

profile of v3, /device:TPU:0, one launch (start us, length us, event | category | flops | bytes accessed | tf_op | source)
XLA Modules:
  0.0 57.8 jit_solution(13542854670094816533)
XLA Ops:
  0.0 56.9 %shard_map.64 = f32[1,3,512,128]{3,2,1,0:T(8,128)S(1)} custom-call(f32[1,3,512,128]{3,2,1,0:T(8,128)} %contributions_hbm.1, s32[1,800]{1,0:T(1,128)} %send_hbm.1, s32[1,800]{1,0:T(1,128)} %arrival_hbm.1, f32[256,128]{1,0:T(8,128)} %diagonal_hbm.1, bf16[256,128,128]{2,1,0:T(8,128)(2,1)} %mortar_hbm.1, bf16[256,128,128]{2,1,0:T(8,128)(2,1)} %inverse_hbm.1), custom_call_target="tpu_custom_call" | custom-call | tf_op jit(solution)/shard_map/pallas_call | solution.py:561
  56.9 0.9 %copy.8 = f32[1,3,512,128]{3,2,1,0:T(8,128)} copy(f32[1,3,512,128]{3,2,1,0:T(8,128)S(1)} %shard_map.64) | data formatting | bytes 1572864

commit v4 on v3

--- a/solution.py
+++ b/solution.py
@@ -220,7 +220,7 @@
         )
 
     live = pl.ds(0, cap)
-    straight_back = tuple(range(1, comps))
+    straight_back = (0,1,2)
 
     def back_planes(c):
         return far_planes[:1] if c in straight_back else far_planes
@@ -326,11 +326,30 @@
             {"narrow": 1 - side},
         )
 
-    def solve(c):
-        with jax.named_scope(f"solve{c}"):
+    def raise_fixes(c):
+        def to_far_hub():
+            for s in range(2):
+                remote(
+                    fix_pair.at[c, s],
+                    up_in.at[c, my_plane, pl.ds(mine, half)],
+                    up_send.at[c],
+                    up_recv.at[c, my_plane],
+                    {"wide": far_hub, "narrow": s},
+                ).start()
+
+        if c in straight_back:
+            pl.when(is_outer)(to_far_hub)
+        else:
+            to_far_hub()
+
+    def await_sums(c):
+        with jax.named_scope(f"await_sums{c}"):
             with jax.named_scope("wait_swap"):
                 swap(c).wait()
             wait_bytes(dense_in.at[c], dense_recv.at[c])
+
+    def solve(c):
+        with jax.named_scope(f"solve{c}"):
 
             def condense(g, carry):
                 first = pl.multiple_of(g * GROUP, GROUP)
@@ -347,21 +366,6 @@
 
             lax.fori_loop(0, half // GROUP, condense, 0, unroll=2)
             swap_back(c).start()
-
-            def to_far_hub():
-                for s in range(2):
-                    remote(
-                        fix_pair.at[c, s],
-                        up_in.at[c, my_plane, pl.ds(mine, half)],
-                        up_send.at[c],
-                        up_recv.at[c, my_plane],
-                        {"wide": far_hub, "narrow": s},
-                    ).start()
-
-            if c in straight_back:
-                pl.when(is_outer)(to_far_hub)
-            else:
-                to_far_hub()
             fixes[c, pl.ds(mine, half), :] = fix_pair[c, side]
 
     def return_own(c):
@@ -499,16 +503,22 @@
     gather_own(0)
     for fetch in fetches:
         fetch.wait()
+    gather_hub(2)
+    await_sums(0)
     solve(0)
-    gather_hub(2)
+    raise_fixes(0)
     gather_own(1)
     return_own(0)
+    await_sums(1)
     solve(1)
+    return_hub(0)
     gather_own(2)
-    return_hub(0)
     return_own(1)
+    await_sums(2)
+    raise_fixes(1)
+    solve(2)
+    raise_fixes(2)
     return_hub(1)
-    solve(2)
     return_own(2)
     return_hub(2)
     place(0)

time: 58 us -> 54.5 us (0.940)
  Pallas kernels: 56.9 us -> 53.4 us
    pallas_call x1, Pallas kernels: 56.9 us -> 53.4 us  [shards(): pl.pallas_call(functools.partial(kernel, n, cap, capp), out_shape=jax.Sha...]
where the time goes in v4:
time: 54.5 us; the launch traced here: 54.3 us
  Pallas kernels  53.4 us (98%)
  local copies, waits for them, and re-layouts  0.88 us (2%)
    pallas_call x1, Pallas kernels, shards(): pl.pallas_call(functools.partial(kernel, n, cap, capp), out_shape=jax.Sha...  53.4 us

profile of v4, /device:TPU:0, one launch (start us, length us, event | category | flops | bytes accessed | tf_op | source)
XLA Modules:
  0.0 54.3 jit_solution(5513258099754055386)
XLA Ops:
  0.0 53.4 %shard_map.64 = f32[1,3,512,128]{3,2,1,0:T(8,128)S(1)} custom-call(f32[1,3,512,128]{3,2,1,0:T(8,128)} %contributions_hbm.1, s32[1,800]{1,0:T(1,128)} %send_hbm.1, s32[1,800]{1,0:T(1,128)} %arrival_hbm.1, f32[256,128]{1,0:T(8,128)} %diagonal_hbm.1, bf16[256,128,128]{2,1,0:T(8,128)(2,1)} %mortar_hbm.1, bf16[256,128,128]{2,1,0:T(8,128)(2,1)} %inverse_hbm.1), custom_call_target="tpu_custom_call" | custom-call | tf_op jit(solution)/shard_map/pallas_call | solution.py:571
  53.4 0.9 %copy.8 = f32[1,3,512,128]{3,2,1,0:T(8,128)} copy(f32[1,3,512,128]{3,2,1,0:T(8,128)S(1)} %shard_map.64) | data formatting | bytes 1572864

commit v5 on v4

--- a/solution.py
+++ b/solution.py
@@ -111,6 +111,7 @@
     ret_send,
     relay_send,
     ret_recv,
+    far_recv,
 ):
     me = lax.axis_index("wide")
     side = lax.axis_index("narrow")
@@ -386,7 +387,7 @@
                             returning_far.at[c, peer, live],
                             returned.at[c, me, live],
                             ret_send.at[c],
-                            ret_recv.at[c],
+                            far_recv.at[c],
                             {"wide": far_base + peer},
                         ).start()
                         return carry
@@ -423,7 +424,7 @@
                             relay.at[c, j, peer, live],
                             returned.at[c, owner, live],
                             relay_send.at[c, j],
-                            ret_recv.at[c],
+                            far_recv.at[c],
                             {"wide": base + peer},
                         ).start()
 
@@ -434,15 +435,23 @@
         with jax.named_scope(f"place{c}"):
             at_hub = len(back_planes(c))
 
+            def half_of(first):
+                columns = pl.ds(pl.multiple_of(first * capp, LANES), slots)
+                rows = returned[c, pl.ds(first, m)].reshape(slots, nodes)
+                return one_hot_dot(place_mask[:, columns], rows)
+
+            wait_bytes(returned.at[c, pl.ds(0, m - 1), live], ret_recv.at[c])
+            out[0, c] = half_of(base)
+
             @pl.when(is_hub)
             def _():
-                wait_bytes(returned.at[c, pl.ds(0, n - 1 - at_hub), live], ret_recv.at[c])
+                wait_bytes(returned.at[c, pl.ds(0, m - at_hub), live], far_recv.at[c])
 
             @pl.when(is_outer)
             def _():
-                wait_bytes(returned.at[c, pl.ds(0, n - 1), live], ret_recv.at[c])
-
-            out[0, c] = one_hot_dot(place_mask[...], returned[c].reshape(n * capp, nodes))
+                wait_bytes(returned.at[c, pl.ds(0, m), live], far_recv.at[c])
+
+            out[0, c] += half_of(far_base)
 
     map_loads[0].wait()
     with jax.named_scope("pick_mask"):
@@ -625,6 +634,7 @@
             dma((comps,)),
             dma((comps, 2)),
             dma((comps,)),
+            dma((comps,)),
         ],
         compiler_params=pltpu.CompilerParams(
             collective_id=0, has_side_effects=True, vmem_limit_bytes=48 * 1024 * 1024

time: 54.5 us -> 54.3 us (level)
  no operation moved by 1% of the time
where the time goes in v5:
time: 54.3 us; the launch traced here: 54.1 us
  Pallas kernels  53.2 us (98%)
  local copies, waits for them, and re-layouts  0.88 us (2%)
    pallas_call x1, Pallas kernels, shards(): pl.pallas_call(functools.partial(kernel, n, cap, capp), out_shape=jax.Sha...  53.2 us

profile of v5, /device:TPU:0, one launch (start us, length us, event | category | flops | bytes accessed | tf_op | source)
XLA Modules:
  0.0 54.1 jit_solution(7652549973345704899)
XLA Ops:
  0.0 53.2 %shard_map.64 = f32[1,3,512,128]{3,2,1,0:T(8,128)S(1)} custom-call(f32[1,3,512,128]{3,2,1,0:T(8,128)} %contributions_hbm.1, s32[1,800]{1,0:T(1,128)} %send_hbm.1, s32[1,800]{1,0:T(1,128)} %arrival_hbm.1, f32[256,128]{1,0:T(8,128)} %diagonal_hbm.1, bf16[256,128,128]{2,1,0:T(8,128)(2,1)} %mortar_hbm.1, bf16[256,128,128]{2,1,0:T(8,128)(2,1)} %inverse_hbm.1), custom_call_target="tpu_custom_call" | custom-call | tf_op jit(solution)/shard_map/pallas_call | solution.py:580
  53.2 0.9 %copy.8 = f32[1,3,512,128]{3,2,1,0:T(8,128)} copy(f32[1,3,512,128]{3,2,1,0:T(8,128)S(1)} %shard_map.64) | data formatting | bytes 1572864
